TPU v7x, 32 devices: a whole 2x2x4 slice. The times are simulated.
32 devices in a mesh: group: 2 (over y), view: 4 (over z), depth: 2 (over x), row: 2 (over core).
Axes of the slice: x: 2, y: 2, z: 4, core: 2. Of those that a mesh axis runs over, the one named last changes fastest.
Arguments:
- features: float32 [4, 32, 8, 512], P('view', None, ('group', 'row')), parts along dimension 2, may hold values from -6 to 6
- cotangent: float32 [8, 32, 8, 512], P('depth', 'view', ('group', 'row')), parts along dimension 2, may hold values from -6 to 6
- src_row: int32 [4, 8, 8, 512], P('view', 'depth', ('group', 'row')), parts along dimension 2, may hold values from -2 to 4, as said below
- src_col: int32 [4, 8, 8, 512], P('view', 'depth', ('group', 'row')), parts along dimension 2, may hold values from 0 to 510
- fractions: int32 [2, 4, 8, 8, 512], P(None, 'view', 'depth', ('group', 'row')), parts along dimension 3, may hold values from 0 to 256
Outputs:
- grad_features: float32 [4, 32, 8, 512], P('view', None, ('group', 'row'), 'depth'), parts along dimension 2
There are 2 independent parts, one for each index of `group`. A program takes and returns all parts, laid end to end along the dimension named above; each array names one. Nothing has to cross between parts.
Inputs may be any that keep to these rules, and one draw needn't show every extreme that they name: src_row[v, d, y, x] lies between y - 2 and y + 1.
All inputs are finite; a program needn't handle non-finite values.
Results may differ from a plain program's by a relative error of at most 0.0003.
Values sent between devices are 32-bit elements; how exact they have to be, the bound alone decides.
A program may use at most 64 MiB of HBM per device.

v0:
```python
import jax
import jax.numpy as jnp
from jax import lax
from jax.sharding import PartitionSpec as P

HALO = 2


def partner(shard, axis, apart):
    return lax.ppermute(shard, axis, [(i, i ^ 1 << apart) for i in range(lax.axis_size(axis))])


def with_halo(block, sides, width):
    for axis, dim in sides:
        count = lax.axis_size(axis)
        forward = [(i, i + 1) for i in range(count - 1)]
        backward = [(target, source) for source, target in forward]
        low = lax.ppermute(
            lax.slice_in_dim(block, block.shape[dim] - width, None, axis=dim), axis, forward
        )
        high = lax.ppermute(lax.slice_in_dim(block, 0, width, axis=dim), axis, backward)
        block = jnp.concatenate([low, block, high], axis=dim)
    return block


def sample(flattened, flat_index, frac_row, frac_col, width):

    def corner(shift_by):
        return jnp.take(flattened, flat_index + shift_by, axis=1)

    upper_mix = (1.0 - frac_col) * corner(0) + frac_col * corner(1)
    lower_mix = (1.0 - frac_col) * corner(width) + frac_col * corner(width + 1)
    mixed = (1.0 - frac_row) * upper_mix + frac_row * lower_mix
    return jnp.transpose(mixed, (1, 0, 2, 3))


def spread(grad_warp, flat_index, frac_row, frac_col, width, length):
    moved = jnp.transpose(grad_warp, (1, 0, 2, 3))
    channels = moved.shape[0]
    upper_part = (1.0 - frac_row) * moved
    lower_part = frac_row * moved
    result = jnp.zeros((channels, length), jnp.float32)
    result = result.at[:, flat_index].add((1.0 - frac_col) * upper_part)
    result = result.at[:, flat_index + 1].add(frac_col * upper_part)
    result = result.at[:, flat_index + width].add((1.0 - frac_col) * lower_part)
    result = result.at[:, flat_index + width + 1].add(frac_col * lower_part)
    return result


def fold_rims(grad_pad):
    upper_rim = grad_pad[:, :HALO]
    lower_rim = grad_pad[:, grad_pad.shape[1] - HALO :]
    interior = grad_pad[:, HALO : grad_pad.shape[1] - HALO]
    is_first = lax.axis_index("row") == 0
    outgoing = jnp.where(is_first, lower_rim, upper_rim)
    incoming = partner(outgoing, "row", 0)
    add_upper = jnp.where(is_first, 0.0, incoming)
    add_lower = jnp.where(is_first, incoming, 0.0)
    interior = interior.at[:, :HALO].add(add_upper)
    interior = interior.at[:, interior.shape[1] - HALO :].add(add_lower)
    return interior


def depth_reduce(partial_grad):
    return lax.psum_scatter(partial_grad, "depth", scatter_dimension=2, tiled=True)


def per_device(features, cotangent, src_row, src_col, fractions):
    channels = features.shape[1]
    row_count = features.shape[2]
    col_count = features.shape[3]
    padded = with_halo(features[0], (("row", 1),), HALO)
    padded_rows = row_count + 2 * HALO
    flattened = padded.reshape(channels, padded_rows * col_count)
    row_offset = lax.axis_index("row") * row_count
    flat_index = (src_row[0] - row_offset + HALO) * col_count + src_col[0]
    weights = fractions[:, 0].astype(jnp.float32) / 256.0
    warped = sample(flattened, flat_index, weights[0], weights[1], col_count)
    view_count = lax.axis_size("view") * features.shape[0]
    factor = 2.0 / view_count
    full_cotangent = lax.all_gather(cotangent, "view", axis=1, tiled=True)
    view_sum = lax.psum(warped, "view")
    average = view_sum / view_count
    grad_warp = factor * full_cotangent * (warped - average)
    spread_out = spread(
        grad_warp, flat_index, weights[0], weights[1], col_count, padded_rows * col_count
    )
    grad_pad = spread_out.reshape(channels, padded_rows, col_count)
    result = fold_rims(depth_reduce(grad_pad))
    return result[None]


def solution(mesh):
    in_specs = (
        P("view", None, ("group", "row"), None),
        P("depth", "view", ("group", "row"), None),
        P("view", "depth", ("group", "row"), None),
        P("view", "depth", ("group", "row"), None),
        P(None, "view", "depth", ("group", "row"), None),
    )
    out_specs = P("view", None, ("group", "row"), "depth")
    return jax.shard_map(
        per_device, mesh=mesh, in_specs=in_specs, out_specs=out_specs, check_vma=False
    )
```

profile of v0, /device:TPU:0, one launch (start us, length us, event | category | flops | bytes accessed | tf_op | source)
XLA Modules:
  0.0 254.8 jit_solution(4598418391159267502)
XLA Ops:
  6.5 2.4 collective-permute-start
  8.9 1.3 collective-permute-start.1
  10.2 0.8 fusion.13
  11.2 0.8 convert_multiply_fusion
  12.4 1.1 pad_maximum_fusion
  13.5 0.5 copy.12
  14.0 14.1 %gather_fusion = f32[4096,32]{1,0:T(8,128)} fusion(f32[32,3072]{0,1:T(8,128)S(1)} %bitcast.135, s32[4096]{0:T(1024)S(1)} %broadcast_clamp_fusion.3), kind=kCustom, calls=%fused_computation.clone | custom fusion | bytes 1064960 | tf_op jit(solution)/shard_map/jit(_take)/gather | solution.py:29
  28.1 1.9 copy.13
  30.0 14.1 %gather_fusion.1 = f32[4096,32]{1,0:T(8,128)} fusion(f32[32,3072]{0,1:T(8,128)S(1)} %bitcast.136, s32[4096]{0:T(1024)S(1)} %broadcast_clamp_fusion.2), kind=kCustom, calls=%fused_computation.1.clone | custom fusion | bytes 1064960 | tf_op jit(solution)/shard_map/jit(_take)/gather | solution.py:29
  44.1 1.9 copy.14
  46.0 14.1 %gather_fusion.2 = f32[4096,32]{1,0:T(8,128)} fusion(f32[32,3072]{0,1:T(8,128)S(1)} %bitcast.137, s32[4096]{0:T(1024)S(1)} %broadcast_clamp_fusion.1), kind=kCustom, calls=%fused_computation.2.clone | custom fusion | bytes 1064960 | tf_op jit(solution)/shard_map/jit(_take)/gather | solution.py:29
  60.1 1.9 copy.15
  62.0 14.1 %gather_fusion.3 = f32[4096,32]{1,0:T(8,128)} fusion(f32[32,3072]{0,1:T(8,128)S(1)} %bitcast.138, s32[4096]{0:T(1024)S(1)} %broadcast_clamp_fusion), kind=kCustom, calls=%fused_computation.3.clone | custom fusion | bytes 1064960 | tf_op jit(solution)/shard_map/jit(_take)/gather | solution.py:29
  76.0 1.9 copy.16
  78.0 1.7 fusion.5
  79.9 22.9 %all_gather.3 = f32[4,32,2,512]{3,2,1,0:T(2,128)S(1)} all-gather(f32[4,8,2,512]{3,2,1,0:T(2,128)S(1)} %copy-done), channel_id=1, replica_groups=mesh['group'=2,'view'=4,'depth'=2,'row'=2] {'view'}, dimensions={1}, use_global_device_ids=true | all-gather | bytes 655360 | tf_op jit(solution)/shard_map/all_gather | solution.py:81
  102.7 22.7 %all-reduce.2.cloned.1.call-done = f32[4,32,2,512]{3,2,1,0:T(2,128)} async-done(((f32[4,32,2,512]{3,2,1,0:T(2,128)}), f32[4,32,2,512]{3,2,1,0:T(2,128)}) %all-reduce.2.cloned.1.call-update) | async-done | bytes 524304 | tf_op jit(solution)/shard_map/psum | solution.py:82
  125.4 1.8 multiply_bitcast_fusion
  127.2 0.6 multiply_bitcast_fusion.1
  127.9 1.8 copy.26
  129.6 1.7 copy.27
  131.4 1.8 copy.28
  133.1 1.7 copy.29
  134.9 23.0 %scatter_custom_fusion = f32[32,3072]{0,1:T(8,128)S(1)} fusion(s32[4096]{0:T(1024)S(1)} %bitcast.158, f32[4096,32]{1,0:T(8,128)} %bitcast.147, f32[]{:T(128)} %constant.99.clone.1), kind=kCustom, calls=%fused_computation.8 | custom fusion | flops 131072 | bytes 393728 | tf_op jit(solution)/shard_map/scatter-add | solution.py:43
  157.9 23.3 %scatter_fusion = f32[32,3072]{0,1:T(8,128)S(1)} fusion(f32[32,3072]{0,1:T(8,128)S(1)} %scatter_custom_fusion, s32[4096]{0:T(1024)S(1)} %bitcast.153, f32[4096,32]{1,0:T(8,128)} %bitcast.142), kind=kCustom, calls=%fused_computation.5 | custom fusion | flops 131072 | bytes 1589248 | tf_op jit(solution)/shard_map/scatter-add | solution.py:44
  181.2 23.3 %scatter_fusion.1 = f32[32,3072]{0,1:T(8,128)S(1)} fusion(f32[32,3072]{0,1:T(8,128)S(1)} %scatter_fusion, s32[4096]{0:T(1024)S(1)} %bitcast.152, f32[4096,32]{1,0:T(8,128)} %bitcast.141), kind=kCustom, calls=%fused_computation.6 | custom fusion | flops 131072 | bytes 1589248 | tf_op jit(solution)/shard_map/scatter-add | solution.py:45
  204.4 23.4 %scatter_fusion.2 = f32[32,3072]{0,1:T(8,128)S(1)} fusion(f32[32,3072]{0,1:T(8,128)S(1)} %scatter_fusion.1, s32[4096]{0:T(1024)S(1)} %bitcast.151, f32[4096,32]{1,0:T(8,128)} %bitcast.140), kind=kCustom, calls=%fused_computation.7 | custom fusion | flops 131072 | bytes 1589248 | tf_op jit(solution)/shard_map/scatter-add | solution.py:46
  227.9 1.5 copy.25
  229.4 14.6 %reduce-scatter.2.cloned.1.call-done = f32[32,6,256]{2,1,0:T(8,128)} async-done(((f32[32,6,512]{2,1,0:T(8,128)}), f32[32,6,256]{2,1,0:T(8,128)}) %reduce-scatter.2.cloned.1.call-update) | async-done | bytes 196624 | tf_op jit(solution)/shard_map/reduce_scatter | solution.py:65
  243.9 1.1 slice_select_fusion
  245.1 1.2 collective-permute-done.2
  246.4 1.6 fusion.9
  (25 shorter events, 0.7 us)
Async XLA Ops:
  6.5 118.9 %all-reduce.2.cloned.1.call-start = ((), (), s32[]{:S(2)}) async-start(), calls=%async_computation.1 | async-start | bytes 1048576 | tf_op jit(solution)/shard_map/psum | solution.py:82
  6.5 5.5 %collective-permute-start = (f32[32,2,512]{2,1,0:T(2,128)}, f32[32,2,512]{2,1,0:T(2,128)S(1)}, u32[]{:S(2)}, u32[]{:S(2)}) collective-permute-start(f32[32,2,512]{2,1,0:T(2,128)} %bitcast.148), channel_id=1, source_target_pairs={{0,1},{2,3},{4,5},{6,7},{8,9},{10,11},{12,13},{14,15},{16,17},{18,... | collective-permute-start | bytes 393224 | tf_op jit(solution)/shard_map/ppermute | solution.py:18
  8.9 3.5 %collective-permute-start.1 = (f32[32,2,512]{2,1,0:T(2,128)}, f32[32,2,512]{2,1,0:T(2,128)S(1)}, u32[]{:S(2)}, u32[]{:S(2)}) collective-permute-start(f32[32,2,512]{2,1,0:T(2,128)} %bitcast.149), channel_id=1, source_target_pairs={{1,0},{3,2},{5,4},{7,6},{9,8},{11,10},{13,12},{15,14},{17,16},{19,... | collective-permute-start | bytes 393224 | tf_op jit(solution)/shard_map/ppermute | solution.py:21
  77.9 1.9 copy-start
  79.7 164.2 %reduce-scatter.2.cloned.1.call-start = ((), (), s32[]{:S(2)}) async-start(), calls=%async_computation.2 | async-start | bytes 786432 | tf_op jit(solution)/shard_map/reduce_scatter | solution.py:65
  245.0 1.3 collective-permute-start.2
Sparse Core Ops, SparseCore 0:
  79.8 45.5 all-reduce.1
  229.5 14.4 reduce-scatter.1
where the time goes:
time: 255 us
  other arithmetic  103 us (40%)
  local copies, waits for them, and re-layouts  72.9 us (29%)
  waiting for transfers between devices  38.9 us (15%)
  blocking collectives  22.9 us (9%)
  between operations  13.7 us (5%)
  starting transfers between devices  3.8 us (1%)
    gather x8, local copies, waits for them, and re-layouts, corner(): return jnp.take(flattened, flat_index + shift_by, axis=1)  63.9 us
    scatter-add x1, other arithmetic, spread(): result = result.at[:, flat_index + width + 1].add(frac_col * lower_part)  23.4 us
    scatter-add x1, other arithmetic, spread(): result = result.at[:, flat_index + 1].add(frac_col * upper_part)  23.3 us
    scatter-add x1, other arithmetic, spread(): result = result.at[:, flat_index + width].add((1.0 - frac_col) * lower_part)  23.3 us
    scatter-add x1, other arithmetic, spread(): result = result.at[:, flat_index].add((1.0 - frac_col) * upper_part)  23 us
    all_gather x1, blocking collectives, per_device(): full_cotangent = lax.all_gather(cotangent, 'view', axis=1, tiled=True)  22.9 us
    psum x1, waiting for transfers between devices, per_device(): view_sum = lax.psum(warped, 'view')  22.7 us
    reduce_scatter x1, waiting for transfers between devices, depth_reduce(): lax.psum_scatter(partial_grad, 'depth', scatter_dimension=2, tiled=True)  14.6 us
  transfers between devices with their start and end apart: 5, of which 4 were waited for; matrix products, arithmetic and copies ran while one was open for 1% of the time, Pallas kernels for 0%

commit v1 on v0

--- a/solution.py
+++ b/solution.py
@@ -78,7 +78,7 @@
     warped = sample(flattened, flat_index, weights[0], weights[1], col_count)
     view_count = lax.axis_size("view") * features.shape[0]
     factor = 2.0 / view_count
-    full_cotangent = lax.all_gather(cotangent, "view", axis=1, tiled=True)
+    full_cotangent = jnp.concatenate(lax.all_gather(cotangent, "view"), axis=1)
     view_sum = lax.psum(warped, "view")
     average = view_sum / view_count
     grad_warp = factor * full_cotangent * (warped - average)

time: 255 us -> 256 us (level)
  no operation moved by 1% of the time
where the time goes in v1:
time: 256 us; the launch traced here: 255 us
  other arithmetic  101 us (39%)
  local copies, waits for them, and re-layouts  75.1 us (29%)
  waiting for transfers between devices  38.8 us (15%)
  blocking collectives  22.9 us (9%)
  between operations  13.7 us (5%)
  starting transfers between devices  3.8 us (1%)
    gather x8, local copies, waits for them, and re-layouts, corner(): return jnp.take(flattened, flat_index + shift_by, axis=1)  65.3 us
    scatter-add x1, other arithmetic, spread(): result = result.at[:, flat_index + width + 1].add(frac_col * lower_part)  23.4 us
    scatter-add x1, other arithmetic, spread(): result = result.at[:, flat_index + 1].add(frac_col * upper_part)  23.3 us
    scatter-add x1, other arithmetic, spread(): result = result.at[:, flat_index + width].add((1.0 - frac_col) * lower_part)  23.3 us
    scatter-add x1, other arithmetic, spread(): result = result.at[:, flat_index].add((1.0 - frac_col) * upper_part)  23 us
    all_gather x1, blocking collectives, per_device(): full_cotangent = jnp.concatenate(lax.all_gather(cotangent, 'view'), axis=1)  22.9 us
    psum x1, waiting for transfers between devices, per_device(): view_sum = lax.psum(warped, 'view')  22.6 us
    reduce_scatter x1, waiting for transfers between devices, depth_reduce(): lax.psum_scatter(partial_grad, 'depth', scatter_dimension=2, tiled=True)  14.6 us
  transfers between devices with their start and end apart: 5, of which 4 were waited for; matrix products, arithmetic and copies ran while one was open for 1% of the time, Pallas kernels for 0%

profile of v1, /device:TPU:0, one launch (start us, length us, event | category | flops | bytes accessed | tf_op | source)
XLA Modules:
  0.0 255.4 jit_solution(15244349749900589649)
XLA Ops:
  6.5 2.4 collective-permute-start
  8.9 1.3 collective-permute-start.1
  10.2 0.8 fusion.13
  11.2 0.8 convert_multiply_fusion
  12.1 0.3 collective-permute-done.1
  12.4 1.1 pad_maximum_fusion
  13.5 0.5 copy.33
  14.0 14.2 %gather_fusion = f32[4096,32]{1,0:T(8,128)} fusion(f32[32,3072]{0,1:T(8,128)S(1)} %bitcast.141, s32[4096]{0:T(1024)S(1)} %broadcast_clamp_fusion.3), kind=kCustom, calls=%fused_computation.clone | custom fusion | bytes 1064960 | tf_op jit(solution)/shard_map/jit(_take)/gather | solution.py:29
  28.1 2.2 copy.34
  30.3 14.2 %gather_fusion.1 = f32[4096,32]{1,0:T(8,128)} fusion(f32[32,3072]{0,1:T(8,128)S(1)} %bitcast.142, s32[4096]{0:T(1024)S(1)} %broadcast_clamp_fusion.2), kind=kCustom, calls=%fused_computation.1.clone | custom fusion | bytes 1064960 | tf_op jit(solution)/shard_map/jit(_take)/gather | solution.py:29
  44.5 2.2 copy.35
  46.6 14.2 %gather_fusion.2 = f32[4096,32]{1,0:T(8,128)} fusion(f32[32,3072]{0,1:T(8,128)S(1)} %bitcast.143, s32[4096]{0:T(1024)S(1)} %broadcast_clamp_fusion.1), kind=kCustom, calls=%fused_computation.2.clone | custom fusion | bytes 1064960 | tf_op jit(solution)/shard_map/jit(_take)/gather | solution.py:29
  60.8 2.2 copy.36
  62.9 14.2 %gather_fusion.3 = f32[4096,32]{1,0:T(8,128)} fusion(f32[32,3072]{0,1:T(8,128)S(1)} %bitcast.144, s32[4096]{0:T(1024)S(1)} %broadcast_clamp_fusion), kind=kCustom, calls=%fused_computation.3.clone | custom fusion | bytes 1064960 | tf_op jit(solution)/shard_map/jit(_take)/gather | solution.py:29
  77.1 2.2 copy.37
  79.3 1.2 fusion.5
  80.6 22.9 %all-gather = f32[16,8,2,512]{3,1,2,0:T(8,128)S(1)} all-gather(f32[4,8,2,512]{3,1,2,0:T(8,128)S(1)} %copy.31), channel_id=2, replica_groups=mesh['group'=2,'view'=4,'depth'=2,'row'=2] {'view'}, dimensions={0}, use_global_device_ids=true | all-gather | bytes 655360 | tf_op jit(solution)/shard_map/all_gather | solution.py:81
  103.5 22.6 %all-reduce.2.cloned.1.call-done = f32[4,32,2,512]{3,1,2,0:T(8,128)} async-done(((f32[4,32,2,512]{3,1,2,0:T(8,128)}), f32[4,32,2,512]{3,1,2,0:T(8,128)}) %all-reduce.2.cloned.1.call-update) | async-done | bytes 524304 | tf_op jit(solution)/shard_map/psum | solution.py:82
  126.2 1.2 multiply_bitcast_fusion
  127.6 2.0 copy.47
  129.6 1.9 copy.48
  131.5 1.9 copy.49
  133.4 1.9 copy.50
  135.4 23.0 %scatter_custom_fusion = f32[32,3072]{0,1:T(8,128)S(1)} fusion(s32[4096]{0:T(1024)S(1)} %bitcast.165, f32[4096,32]{1,0:T(8,128)} %bitcast.153, f32[]{:T(128)} %constant.99.clone.1), kind=kCustom, calls=%fused_computation.8 | custom fusion | flops 131072 | bytes 393728 | tf_op jit(solution)/shard_map/scatter-add | solution.py:43
  158.4 23.3 %scatter_fusion = f32[32,3072]{0,1:T(8,128)S(1)} fusion(f32[32,3072]{0,1:T(8,128)S(1)} %scatter_custom_fusion, s32[4096]{0:T(1024)S(1)} %bitcast.160, f32[4096,32]{1,0:T(8,128)} %bitcast.148), kind=kCustom, calls=%fused_computation.5 | custom fusion | flops 131072 | bytes 1589248 | tf_op jit(solution)/shard_map/scatter-add | solution.py:44
  181.7 23.3 %scatter_fusion.1 = f32[32,3072]{0,1:T(8,128)S(1)} fusion(f32[32,3072]{0,1:T(8,128)S(1)} %scatter_fusion, s32[4096]{0:T(1024)S(1)} %bitcast.159, f32[4096,32]{1,0:T(8,128)} %bitcast.147), kind=kCustom, calls=%fused_computation.6 | custom fusion | flops 131072 | bytes 1589248 | tf_op jit(solution)/shard_map/scatter-add | solution.py:45
  204.9 23.4 %scatter_fusion.2 = f32[32,3072]{0,1:T(8,128)S(1)} fusion(f32[32,3072]{0,1:T(8,128)S(1)} %scatter_fusion.1, s32[4096]{0:T(1024)S(1)} %bitcast.158, f32[4096,32]{1,0:T(8,128)} %bitcast.146), kind=kCustom, calls=%fused_computation.7 | custom fusion | flops 131072 | bytes 1589248 | tf_op jit(solution)/shard_map/scatter-add | solution.py:46
  228.4 1.4 copy.46
  229.9 14.6 %reduce-scatter.2.cloned.1.call-done = f32[32,6,256]{2,1,0:T(8,128)} async-done(((f32[32,6,512]{2,1,0:T(8,128)}), f32[32,6,256]{2,1,0:T(8,128)}) %reduce-scatter.2.cloned.1.call-update) | async-done | bytes 196624 | tf_op jit(solution)/shard_map/reduce_scatter | solution.py:65
  244.5 1.1 slice_select_fusion
  245.6 1.2 collective-permute-done.2
  246.9 1.6 fusion.9
  (29 shorter events, 0.7 us)
Async XLA Ops:
  6.5 119.6 %all-reduce.2.cloned.1.call-start = ((), (), s32[]{:S(2)}) async-start(), calls=%async_computation.1 | async-start | bytes 1048576 | tf_op jit(solution)/shard_map/psum | solution.py:82
  6.5 5.5 %collective-permute-start = (f32[32,2,512]{2,1,0:T(2,128)}, f32[32,2,512]{2,1,0:T(2,128)S(1)}, u32[]{:S(2)}, u32[]{:S(2)}) collective-permute-start(f32[32,2,512]{2,1,0:T(2,128)} %bitcast.155), channel_id=1, source_target_pairs={{0,1},{2,3},{4,5},{6,7},{8,9},{10,11},{12,13},{14,15},{16,17},{18,... | collective-permute-start | bytes 393224 | tf_op jit(solution)/shard_map/ppermute | solution.py:18
  8.9 3.5 %collective-permute-start.1 = (f32[32,2,512]{2,1,0:T(2,128)}, f32[32,2,512]{2,1,0:T(2,128)S(1)}, u32[]{:S(2)}, u32[]{:S(2)}) collective-permute-start(f32[32,2,512]{2,1,0:T(2,128)} %bitcast.156), channel_id=1, source_target_pairs={{1,0},{3,2},{5,4},{7,6},{9,8},{11,10},{13,12},{15,14},{17,16},{19,... | collective-permute-start | bytes 393224 | tf_op jit(solution)/shard_map/ppermute | solution.py:21
  79.3 1.3 copy-start.1
  80.4 45.7 %copy-start = (f32[4,32,2,512]{3,1,2,0:T(8,128)S(1)}, f32[4,32,2,512]{3,1,2,0:T(8,128)}, u32[]{:S(2)}) copy-start(f32[4,32,2,512]{3,1,2,0:T(8,128)} %fusion.5) | copy-start | bytes 1572868
  80.4 164.0 %reduce-scatter.2.cloned.1.call-start = ((), (), s32[]{:S(2)}) async-start(), calls=%async_computation.2 | async-start | bytes 786432 | tf_op jit(solution)/shard_map/reduce_scatter | solution.py:65
  245.6 1.3 collective-permute-start.2
Sparse Core Ops, SparseCore 0:
  80.6 45.5 all-reduce.1
  230.0 14.4 reduce-scatter.1
